TPU v7x, 32 devices: a whole 2x2x4 slice. The times are simulated.
32 devices in a mesh: wide: 16 (over z, y, x), narrow: 2 (over core).
Axes of the slice: x: 2, y: 2, z: 4, core: 2. Of those that a mesh axis runs over, the one named last changes fastest.
Arguments:
- contributions: float32 [2, 3, 8192, 128], P('narrow', None, 'wide'), may hold values from -6 to 6
- send_map: int32 [16, 800], P('wide'), may hold values from -1 to 511, as said below
- arrival_map: int32 [16, 800], P('wide'), may hold values from -1 to 255, as said below
- dual_diagonal: float32 [4096, 128], P('wide'), may hold values from 0.5 to 2
- mortar: bfloat16 [4096, 128, 128], P('wide'), may hold values from -0.5 to 0.5
- master_inverse: bfloat16 [4096, 128, 128], P('wide'), may hold values from -0.5 to 0.5
Outputs:
- corrections: float32 [2, 3, 8192, 128], P('narrow', None, 'wide')
Inputs may be any that keep to these rules, and one draw needn't show every extreme that they name: `send_map`: each row 0 to 511 of a partition stands in exactly one of its slots. Some stripe has all 50 of its slots used by every partition. arrival_map[d, o * 50 + c] is -1 exactly where send_map[o, d * 50 + c] is -1.
All inputs are finite; a program needn't handle non-finite values.
Results may differ from a plain program's by a relative error of at most 0.0041.
Values sent between devices are 32-bit elements; how exact they have to be, the bound alone decides.
No kernel may reach another device: no remote copies, remote signals or barrier semaphores. Data moves between devices by JAX's collectives and lax.ppermute only.
A program may use at most 64 MiB of HBM per device.

v0:
```python
import jax
import jax.numpy as jnp
from jax import lax
from jax.sharding import PartitionSpec as P


def partner_2(value, axis, stride):
    mask = 2**stride
    pairs = [(source, source ^ mask) for source in range(lax.axis_size(axis))]
    return lax.ppermute(value, axis, pairs)


def condense(slave_sums, master_sums, diagonal, mortar_part, inverse_part):
    multiplier_low = (slave_sums / diagonal[None]).astype(jnp.bfloat16)
    pushed = jnp.einsum(
        "bij,cbi->cbj", mortar_part, multiplier_low, preferred_element_type=jnp.float32
    )
    condensed_low = (master_sums + pushed).astype(jnp.bfloat16)
    master_fix = jnp.einsum(
        "bkj,cbj->cbk", inverse_part, condensed_low, preferred_element_type=jnp.float32
    )
    master_low = master_fix.astype(jnp.bfloat16)
    slave_fix = (
        jnp.einsum("bij,cbj->cbi", mortar_part, master_low, preferred_element_type=jnp.float32)
        / diagonal[None]
    )
    return (slave_fix, master_fix)


def shards(contributions, send_map, arrival_map, dual_diagonal, mortar, master_inverse):
    my_side = lax.axis_index("narrow")
    block_count = dual_diagonal.shape[0]
    node_count = contributions.shape[3]
    comp_count = contributions.shape[1]
    row_count = contributions.shape[2]
    picked = send_map[0]
    is_live = picked >= 0
    filled = jnp.where(is_live, picked, 0)
    outgoing = jnp.take(contributions[0], filled, axis=1) * is_live[None, :, None].astype(
        jnp.float32
    )
    landing = jnp.where(is_live, picked, row_count)
    block_ids = jnp.arange(block_count, dtype=jnp.int32)
    received_rows = lax.all_to_all(outgoing, "wide", split_axis=1, concat_axis=1, tiled=True)
    choosing_mask = (arrival_map[0][:, None] == block_ids[None, :]).astype(jnp.float32)
    local_row_sums = jnp.einsum(
        "gxp,xt->gtp", received_rows, choosing_mask, precision=lax.Precision.HIGHEST
    )
    partner = partner_2(local_row_sums, "narrow", 0)
    slave_sums = jnp.where(my_side == 0, local_row_sums, partner)
    master_sums = jnp.where(my_side == 0, partner, local_row_sums)
    slave_fix, master_fix = condense(slave_sums, master_sums, dual_diagonal, mortar, master_inverse)
    local_correction = jnp.where(my_side == 0, slave_fix, master_fix)
    departing_rows = jnp.einsum(
        "oxq,ux->ouq", local_correction, choosing_mask, precision=lax.Precision.HIGHEST
    )
    returned = lax.all_to_all(departing_rows, "wide", split_axis=1, concat_axis=1, tiled=True)
    placed = (
        jnp.zeros((comp_count, row_count + 1, node_count), jnp.float32)
        .at[:, landing, :]
        .set(returned)
    )
    return placed[:, :row_count][None]


def solution(mesh):
    placed = (
        P("narrow", None, "wide", None),
        P("wide", None),
        P("wide", None),
        P("wide", None),
        P("wide", None, None),
        P("wide", None, None),
    )
    return jax.shard_map(
        shards,
        mesh=mesh,
        in_specs=placed,
        out_specs=P("narrow", None, "wide", None),
        check_vma=False,
    )
```

profile of v0, /device:TPU:0, one launch (start us, length us, event | category | flops | bytes accessed | tf_op | source)
XLA Modules:
  0.0 153.0 jit_solution(14585886316772614351)
XLA Ops:
  0.0 0.7 fusion.21
  0.7 0.7 reduce.2
  1.5 1.7 %copy.37 = f32[1,3,512,128]{3,1,2,0:T(4,128)S(1)} copy(f32[1,3,512,128]{3,2,1,0:T(8,128)} %param.6) | data formatting | bytes 1572864 | tf_op args[0]
  3.1 3.6 %gather_fusion = f32[800,3,128]{2,1,0:T(4,128)S(1)} fusion(f32[3,512,128]{2,0,1:T(4,128)S(1)} %bitcast.35, s32[1024]{0:T(1024)S(1)} %pad_clamp_fusion), kind=kCustom, calls=%fused_computation | custom fusion | bytes 2460800 | tf_op jit(solution)/shard_map/jit(_take)/gather | solution.py:39
  6.8 5.0 %multiply_bitcast_fusion = f32[3,800,128]{2,0,1:T(4,128)} fusion(f32[800,3,128]{2,1,0:T(4,128)S(1)} %gather_fusion, f32[800]{0:T(1024)S(1)} %get-tuple-element.8, pred[800]{0:T(1024)(128)(4,1)S(1)} %get-tuple-element.7), kind=kLoop, calls=%fused_computation.2 | loop fusion | flops 614400 | bytes 2461600 | tf_op jit(solution)/shard_map/mul | solution.py:39
  11.8 0.0 copy-start.1
  11.8 8.5 %all-to-all-start = ((f32[3,800,128]{2,0,1:T(4,128)}), f32[3,800,128]{2,0,1:T(4,128)S(1)}, u32[]{:S(2)}, u32[]{:S(2)}) async-start(f32[3,800,128]{2,0,1:T(4,128)} %multiply_bitcast_fusion), calls=%async_computation | async-start | bytes 3276800 | tf_op jit(solution)/shard_map/all_to_all | solution.py:44
  20.3 0.0 copy-done.1
  20.3 0.0 copy-start
  20.3 35.2 %all-to-all-done = f32[3,800,128]{2,0,1:T(4,128)S(1)} async-done(((f32[3,800,128]{2,0,1:T(4,128)}), f32[3,800,128]{2,0,1:T(4,128)S(1)}, u32[]{:S(2)}, u32[]{:S(2)}) %all-to-all-start) | async-done | bytes 1228832 | tf_op jit(solution)/shard_map/all_to_all | solution.py:44
  55.5 1.2 fusion.4
  56.7 0.1 collective-permute-start
  56.8 1.7 %collective-permute-done = f32[3,256,128]{2,1,0:T(8,128)S(1)} collective-permute-done((f32[3,256,128]{2,1,0:T(8,128)S(1)}, f32[3,256,128]{2,1,0:T(8,128)S(1)}, u32[]{:S(2)}, u32[]{:S(2)}) %collective-permute-start) | collective-permute-done | bytes 393248 | tf_op jit(solution)/shard_map/ppermute | solution.py:10
  58.5 0.0 copy-done
  58.5 0.1 divide_convert_fusion
  58.5 0.0 slice-start
  58.5 5.8 %fusion.17 = f32[256,3,128]{2,1,0:T(4,128)S(1)} fusion(bf16[256,128,128]{2,1,0:T(8,128)(2,1)} %param.10, bf16[3,256,128]{2,1,0:T(8,128)(2,1)S(1)} %divide_convert_fusion), kind=kOutput, calls=%fused_computation.23 | convolution fusion | flops 25165824 | bytes 8978432 | tf_op jit(solution)/shard_map/bij,cbi->cbj/dot_general | solution.py:15
  64.3 0.0 slice-start.1
  64.3 0.1 fusion.12
  64.4 7.9 %fusion.15 = f32[256,3,128]{2,1,0:T(4,128)S(1)} fusion(bf16[256,128,128]{2,1,0:T(8,128)(2,1)} %param.11, bf16[3,256,128]{2,1,0:T(8,128)(2,1)S(1)} %fusion.12), kind=kOutput, calls=%fused_computation.21 | convolution fusion | flops 25165824 | bytes 8978432 | tf_op jit(solution)/shard_map/bkj,cbj->cbk/dot_general | solution.py:19
  72.4 0.0 slice-done
  72.4 0.0 slice-done.1
  72.4 4.4 %fusion.1 = f32[3,256,128]{2,0,1:T(4,128)S(1)} fusion(f32[256,3,128]{2,1,0:T(4,128)S(1)} %fusion.15, bf16[256,128,128]{2,1,0:T(8,128)(2,1)S(1)} %bitcast.33, f32[256,128]{1,0:T(8,128)S(1)} %copy-done, pred[]{:T(512)S(6)} %eq.24), kind=kOutput, calls=%fused_computation.6 | convolution fusion | flops 25460736 | bytes 9306113 | tf_op jit(solution)/shard_map/bij,cbj->cbi/dot_general | solution.py:24
  76.8 0.9 convolution_bitcast_fusion
  77.7 0.8 copy.23
  78.6 48.1 %all_to_all.10 = f32[3,800,128]{2,0,1:T(4,128)S(1)} all-to-all(f32[3,800,128]{2,0,1:T(4,128)S(1)} %copy.23), channel_id=1, replica_groups=mesh['wide'=16,'narrow'=2] {'wide'}, dimensions={1} | all-to-all | bytes 2457600 | tf_op jit(solution)/shard_map/all_to_all | solution.py:57
  126.6 0.1 broadcast_in_dim.28
  126.8 25.1 %scatter_fusion = f32[3,513,128]{2,0,1:T(4,128)S(1)} fusion(f32[3,513,128]{2,0,1:T(4,128)S(1)} %broadcast_in_dim.28, s32[800]{0:T(1024)S(1)} %get-tuple-element.6, f32[800,3,128]{2,1,0:T(4,128)S(1)} %bitcast.34), kind=kCustom, calls=%fused_computation.1 | custom fusion | bytes 3689600 | tf_op jit(solution)/shard_map/scatter | solution.py:61
  151.9 0.2 slice_bitcast_fusion
  152.1 0.9 copy.24
  (4 shorter events, 0.0 us)
Async XLA Ops:
  11.8 8.5 %copy-start.1 = (s32[1,800]{1,0:T(1,128)S(1)}, s32[1,800]{1,0:T(1,128)}, u32[]{:S(2)}) copy-start(s32[1,800]{1,0:T(1,128)} %param.8) | copy-start | bytes 9604
  11.8 43.7 %all-to-all-start = ((f32[3,800,128]{2,0,1:T(4,128)}), f32[3,800,128]{2,0,1:T(4,128)S(1)}, u32[]{:S(2)}, u32[]{:S(2)}) async-start(f32[3,800,128]{2,0,1:T(4,128)} %multiply_bitcast_fusion), calls=%async_computation | async-start | bytes 3276800 | tf_op jit(solution)/shard_map/all_to_all | solution.py:44
  20.3 38.2 %copy-start = (f32[256,128]{1,0:T(8,128)S(1)}, f32[256,128]{1,0:T(8,128)}, u32[]{:S(2)}) copy-start(f32[256,128]{1,0:T(8,128)} %param.9) | copy-start | bytes 393220
  56.7 1.8 %collective-permute-start = (f32[3,256,128]{2,1,0:T(8,128)S(1)}, f32[3,256,128]{2,1,0:T(8,128)S(1)}, u32[]{:S(2)}, u32[]{:S(2)}) collective-permute-start(f32[3,256,128]{2,1,0:T(8,128)S(1)} %fusion.4), channel_id=1, source_target_pairs={{0,1},{1,0},{2,3},{3,2},{4,5},{5,4},{6,7},{7,6},{8,9},{9,8},{10,11... | collective-permute-start | bytes 1179656 | tf_op jit(solution)/shard_map/ppermute | solution.py:10
  58.5 13.8 %slice-start = ((s8[8388608]{0:T(1024)(128)(4,1)}), s8[4194304]{0:T(1024)(128)(4,1)S(1)}, s32[]{:S(2)}) async-start(s8[8388608]{0:T(1024)(128)(4,1)} %bitcast.32), calls=%async_computation.2 | async-start | bytes 8388608
  64.3 8.0 %slice-start.1 = ((s8[8388608]{0:T(1024)(128)(4,1)}), s8[4194304]{0:T(1024)(128)(4,1)S(1)}, s32[]{:S(2)}) async-start(s8[8388608]{0:T(1024)(128)(4,1)} %bitcast.32), calls=%async_computation.3 | async-start | bytes 8388608
where the time goes:
time: 153 us
  blocking collectives  48.1 us (31%)
  waiting for transfers between devices  36.9 us (24%)
  local copies, waits for them, and re-layouts  32.5 us (21%)
  matrix products  20.3 us (13%)
  starting transfers between devices  8.54 us (6%)
  other arithmetic  6.57 us (4%)
    all_to_all x1, blocking collectives, shards(): lax.all_to_all(departing_rows, 'wide', split_axis=1, concat_axis=1, tiled...  48.1 us
    all_to_all x1, waiting for transfers between devices, shards(): lax.all_to_all(outgoing, 'wide', split_axis=1, concat_axis=1, tiled=True)  35.2 us
    scatter x1, local copies, waits for them, and re-layouts, shards(): placed = jnp.zeros((comp_count, row_count + 1, node_count), jnp.float32)....  25.1 us
    all_to_all x1, starting transfers between devices, shards(): lax.all_to_all(outgoing, 'wide', split_axis=1, concat_axis=1, tiled=True)  8.47 us
    dot_general x1, matrix products, condense(): jnp.einsum('bkj,cbj->cbk', inverse_part, condensed_low, preferred_element...  7.93 us
    dot_general x1, matrix products, condense(): jnp.einsum('bij,cbi->cbj', mortar_part, multiplier_low, preferred_element...  5.8 us
    mul x1, other arithmetic, shards(): jnp.take(contributions[0], filled, axis=1)  4.99 us
    dot_general x1, matrix products, condense(): jnp.einsum('bij,cbj->cbi', mortar_part, master_low, preferred_element_typ...  4.45 us
  transfers between devices with their start and end apart: 2, of which 2 were waited for; matrix products, arithmetic and copies ran while one was open for 0% of the time, Pallas kernels for 0%

commit v1 on v0

--- a/solution.py
+++ b/solution.py
@@ -54,7 +54,12 @@
     departing_rows = jnp.einsum(
         "oxq,ux->ouq", local_correction, choosing_mask, precision=lax.Precision.HIGHEST
     )
-    returned = lax.all_to_all(departing_rows, "wide", split_axis=1, concat_axis=1, tiled=True)
+    returned = jnp.concatenate(
+        lax.all_to_all(
+            jnp.stack(jnp.split(departing_rows, lax.axis_size("wide"), axis=1)), "wide", 0, 0
+        ),
+        axis=1,
+    )
     placed = (
         jnp.zeros((comp_count, row_count + 1, node_count), jnp.float32)
         .at[:, landing, :]

time: 153 us -> 147 us (0.961)
  blocking collectives: 48.1 us -> 41.9 us
    all_to_all x1, blocking collectives: 48.1 us -> 41.9 us  [shards(): lax.all_to_all(jnp.stack(jnp.split(departing_rows, lax.axis_size('wide'),...]
where the time goes in v1:
time: 147 us; the launch traced here: 146 us
  blocking collectives  41.9 us (29%)
  waiting for transfers between devices  36.9 us (25%)
  local copies, waits for them, and re-layouts  32.5 us (22%)
  matrix products  20.3 us (14%)
  starting transfers between devices  8.54 us (6%)
  other arithmetic  5.95 us (4%)
    all_to_all x1, blocking collectives, shards(): lax.all_to_all(jnp.stack(jnp.split(departing_rows, lax.axis_size('wide'),...  41.9 us
    all_to_all x1, waiting for transfers between devices, shards(): lax.all_to_all(outgoing, 'wide', split_axis=1, concat_axis=1, tiled=True)  35.2 us
    scatter x1, local copies, waits for them, and re-layouts, shards(): placed = jnp.zeros((comp_count, row_count + 1, node_count), jnp.float32)....  24.8 us
    all_to_all x1, starting transfers between devices, shards(): lax.all_to_all(outgoing, 'wide', split_axis=1, concat_axis=1, tiled=True)  8.47 us
    dot_general x1, matrix products, condense(): jnp.einsum('bkj,cbj->cbk', inverse_part, condensed_low, preferred_element...  7.93 us
    dot_general x1, matrix products, condense(): jnp.einsum('bij,cbi->cbj', mortar_part, multiplier_low, preferred_element...  5.8 us
    mul x1, other arithmetic, shards(): jnp.take(contributions[0], filled, axis=1)  4.99 us
    dot_general x1, matrix products, condense(): jnp.einsum('bij,cbj->cbi', mortar_part, master_low, preferred_element_typ...  4.45 us
  transfers between devices with their start and end apart: 2, of which 2 were waited for; matrix products, arithmetic and copies ran while one was open for 0% of the time, Pallas kernels for 0%

profile of v1, /device:TPU:0, one launch (start us, length us, event | category | flops | bytes accessed | tf_op | source)
XLA Modules:
  0.0 146.4 jit_solution(4216280213869555110)
XLA Ops:
  0.0 0.0 copy-start.1
  0.0 0.8 fusion.37
  0.8 1.7 %copy.38 = f32[1,3,512,128]{3,1,2,0:T(4,128)S(1)} copy(f32[1,3,512,128]{3,2,1,0:T(8,128)} %param.6) | data formatting | bytes 1572864 | tf_op args[0]
  2.5 0.0 copy-done.1
  2.5 3.6 %gather_fusion = f32[800,3,128]{2,1,0:T(4,128)S(1)} fusion(f32[3,512,128]{2,0,1:T(4,128)S(1)} %bitcast.99, s32[1024]{0:T(1024)S(1)} %pad_clamp_fusion), kind=kCustom, calls=%fused_computation | custom fusion | bytes 2460800 | tf_op jit(solution)/shard_map/jit(_take)/gather | solution.py:39
  6.2 5.0 %multiply_bitcast_fusion = f32[3,800,128]{2,0,1:T(4,128)} fusion(f32[800,3,128]{2,1,0:T(4,128)S(1)} %gather_fusion, f32[800]{0:T(1024)S(1)} %get-tuple-element.8, pred[800]{0:T(1024)(128)(4,1)S(1)} %get-tuple-element.7), kind=kLoop, calls=%fused_computation.2 | loop fusion | flops 614400 | bytes 2461600 | tf_op jit(solution)/shard_map/mul | solution.py:39
  11.2 0.0 copy-start.2
  11.2 8.5 %all-to-all-start = ((f32[3,800,128]{2,0,1:T(4,128)}), f32[3,800,128]{2,0,1:T(4,128)S(1)}, u32[]{:S(2)}, u32[]{:S(2)}) async-start(f32[3,800,128]{2,0,1:T(4,128)} %multiply_bitcast_fusion), calls=%async_computation | async-start | bytes 3276800 | tf_op jit(solution)/shard_map/all_to_all | solution.py:44
  19.7 0.0 copy-done.2
  19.7 0.0 copy-start
  19.7 35.2 %all-to-all-done = f32[3,800,128]{2,0,1:T(4,128)S(1)} async-done(((f32[3,800,128]{2,0,1:T(4,128)}), f32[3,800,128]{2,0,1:T(4,128)S(1)}, u32[]{:S(2)}, u32[]{:S(2)}) %all-to-all-start) | async-done | bytes 1228832 | tf_op jit(solution)/shard_map/all_to_all | solution.py:44
  54.9 1.2 fusion.4
  56.1 0.1 collective-permute-start
  56.2 1.7 %collective-permute-done = f32[3,256,128]{2,1,0:T(8,128)S(1)} collective-permute-done((f32[3,256,128]{2,1,0:T(8,128)S(1)}, f32[3,256,128]{2,1,0:T(8,128)S(1)}, u32[]{:S(2)}, u32[]{:S(2)}) %collective-permute-start) | collective-permute-done | bytes 393248 | tf_op jit(solution)/shard_map/ppermute | solution.py:10
  57.9 0.0 copy-done
  57.9 0.1 divide_convert_fusion
  57.9 0.0 slice-start
  57.9 5.8 %fusion.17 = f32[256,3,128]{2,1,0:T(4,128)S(1)} fusion(bf16[256,128,128]{2,1,0:T(8,128)(2,1)} %param.10, bf16[3,256,128]{2,1,0:T(8,128)(2,1)S(1)} %divide_convert_fusion), kind=kOutput, calls=%fused_computation.23 | convolution fusion | flops 25165824 | bytes 8978432 | tf_op jit(solution)/shard_map/bij,cbi->cbj/dot_general | solution.py:15
  63.7 0.0 slice-start.1
  63.7 0.1 fusion.12
  63.8 7.9 %fusion.15 = f32[256,3,128]{2,1,0:T(4,128)S(1)} fusion(bf16[256,128,128]{2,1,0:T(8,128)(2,1)} %param.11, bf16[3,256,128]{2,1,0:T(8,128)(2,1)S(1)} %fusion.12), kind=kOutput, calls=%fused_computation.21 | convolution fusion | flops 25165824 | bytes 8978432 | tf_op jit(solution)/shard_map/bkj,cbj->cbk/dot_general | solution.py:19
  71.8 0.0 slice-done
  71.8 0.0 slice-done.1
  71.8 4.4 %fusion.1 = f32[3,256,128]{2,0,1:T(4,128)S(1)} fusion(f32[256,3,128]{2,1,0:T(4,128)S(1)} %fusion.15, bf16[256,128,128]{2,1,0:T(8,128)(2,1)S(1)} %bitcast.97, f32[256,128]{1,0:T(8,128)S(1)} %copy-done, pred[]{:T(512)S(6)} %eq.24), kind=kOutput, calls=%fused_computation.6 | convolution fusion | flops 25460736 | bytes 9306113 | tf_op jit(solution)/shard_map/bij,cbj->cbi/dot_general | solution.py:24
  76.2 0.9 convolution_bitcast_fusion
  77.4 41.9 %all_to_all.10 = f32[16,3,50,128]{3,2,1,0:T(8,128)S(1)} all-to-all(f32[16,3,50,128]{3,2,1,0:T(8,128)S(1)} %fusion.20), channel_id=1, replica_groups=mesh['wide'=16,'narrow'=2] {'wide'}, dimensions={0} | all-to-all | bytes 2457600 | tf_op jit(solution)/shard_map/all_to_all | solution.py:58
  119.3 0.1 copy.23
  119.4 0.1 reshape.82
  119.5 0.8 copy.24
  120.4 0.1 broadcast_in_dim.28
  120.5 24.8 %scatter_fusion = f32[3,513,128]{2,0,1:T(4,128)S(1)} fusion(f32[3,513,128]{2,0,1:T(4,128)S(1)} %broadcast_in_dim.28, s32[800]{0:T(1024)S(1)} %get-tuple-element.6, f32[800,3,128]{2,1,0:T(4,128)S(1)} %copy.24), kind=kCustom, calls=%fused_computation.1 | custom fusion | bytes 3689600 | tf_op jit(solution)/shard_map/scatter | solution.py:66
  145.3 0.2 slice_bitcast_fusion
  145.5 0.9 copy.25
  (21 shorter events, 0.2 us)
Async XLA Ops:
  0.0 2.5 %copy-start.1 = (s32[1,800]{1,0:T(1,128)S(1)}, s32[1,800]{1,0:T(1,128)}, u32[]{:S(2)}) copy-start(s32[1,800]{1,0:T(1,128)} %param.7) | copy-start | bytes 9604
  11.2 8.5 %copy-start.2 = (s32[1,800]{1,0:T(1,128)S(1)}, s32[1,800]{1,0:T(1,128)}, u32[]{:S(2)}) copy-start(s32[1,800]{1,0:T(1,128)} %param.8) | copy-start | bytes 9604
  11.2 43.7 %all-to-all-start = ((f32[3,800,128]{2,0,1:T(4,128)}), f32[3,800,128]{2,0,1:T(4,128)S(1)}, u32[]{:S(2)}, u32[]{:S(2)}) async-start(f32[3,800,128]{2,0,1:T(4,128)} %multiply_bitcast_fusion), calls=%async_computation | async-start | bytes 3276800 | tf_op jit(solution)/shard_map/all_to_all | solution.py:44
  19.7 38.2 %copy-start = (f32[256,128]{1,0:T(8,128)S(1)}, f32[256,128]{1,0:T(8,128)}, u32[]{:S(2)}) copy-start(f32[256,128]{1,0:T(8,128)} %param.9) | copy-start | bytes 393220
  56.1 1.8 %collective-permute-start = (f32[3,256,128]{2,1,0:T(8,128)S(1)}, f32[3,256,128]{2,1,0:T(8,128)S(1)}, u32[]{:S(2)}, u32[]{:S(2)}) collective-permute-start(f32[3,256,128]{2,1,0:T(8,128)S(1)} %fusion.4), channel_id=1, source_target_pairs={{0,1},{1,0},{2,3},{3,2},{4,5},{5,4},{6,7},{7,6},{8,9},{9,8},{10,11... | collective-permute-start | bytes 1179656 | tf_op jit(solution)/shard_map/ppermute | solution.py:10
  57.9 13.8 %slice-start = ((s8[8388608]{0:T(1024)(128)(4,1)}), s8[4194304]{0:T(1024)(128)(4,1)S(1)}, s32[]{:S(2)}) async-start(s8[8388608]{0:T(1024)(128)(4,1)} %bitcast.96), calls=%async_computation.2 | async-start | bytes 8388608
  63.7 8.0 %slice-start.1 = ((s8[8388608]{0:T(1024)(128)(4,1)}), s8[4194304]{0:T(1024)(128)(4,1)S(1)}, s32[]{:S(2)}) async-start(s8[8388608]{0:T(1024)(128)(4,1)} %bitcast.96), calls=%async_computation.3 | async-start | bytes 8388608
